TPU v7x, 32 devices: a whole 2x2x4 slice. The times are simulated.
32 devices in a mesh: table: 4 (over y, core), batch: 8 (over z, x).
Axes of the slice: x: 2, y: 2, z: 4, core: 2. Of those that a mesh axis runs over, the one named last changes fastest.
Arguments:
- emb: bfloat16 [4, 262144, 128], P('table', 'batch'), may hold values from -6 to 6
- short_rows: int32 [192, 4, 32], P(('table', 'batch')), may hold values from 0 to 262143
- short_len: int32 [192, 4], P(('table', 'batch')), may hold values from 1 to 32
- short_sample: int32 [192, 4], P(('table', 'batch')), may hold values from 0 to 7, as said below
- long_rows: int32 [64, 4, 512], P(('table', 'batch')), may hold values from 0 to 262143, as said below
- long_len: int32 [64, 4], P(('table', 'batch')), may hold values from 33 to 500, as said below
- long_sample: int32 [64, 4], P(('table', 'batch')), may hold values from 0 to 7, as said below
Outputs:
- pooled: float32 [256, 4, 128], P(('table', 'batch'))
Inputs may be any that keep to these rules, and one draw needn't show every extreme that they name: For each block of 6 short bags and 2 long bags with the same j // 6 and j // 2, and each table, short_sample and long_sample together name each of the 8 samples exactly once. `long_sample`: see short_sample. `long_rows`: within one bag no row id stands more than 256 times among the first long_len positions, and in every draw some bag has a row id that stands exactly that often. `long_len`: in every draw some long bag has length 500.
All inputs are finite; a program needn't handle non-finite values.
Results may differ from a plain program's by a relative error of at most 0.0003.
Values sent between devices are 32-bit elements; how exact they have to be, the bound alone decides.
No kernel may reach another device: no remote copies, remote signals or barrier semaphores. Data moves between devices by JAX's collectives and lax.ppermute only.
A program may use at most 64 MiB of HBM per device.

v0:
```python
import jax
import jax.numpy as jnp
from jax import lax
from jax.sharding import PartitionSpec as P


def mask_rows(rows, lengths):
    place = lax.broadcasted_iota(jnp.int32, rows.shape, 2)
    return jnp.where(place < lengths[:, :, None], rows, -1)


def pool_rows(keys, table, row_base):
    bag_count = keys.shape[0]
    rows_dev = table.shape[0]
    block = min(8192, rows_dev)
    high_count = block // 128
    local = keys - row_base
    inside = (local >= 0) & (local < rows_dev)
    high = jnp.where(inside, local // 128, -1)
    low = jnp.where(inside, local % 128, -1)
    low_hot = (low[:, :, None] == lax.broadcasted_iota(jnp.int32, (1, 1, 128), 2)).astype(
        jnp.bfloat16
    )

    def add_block(index, total):
        targets = index * high_count + lax.broadcasted_iota(jnp.int32, (1, 1, high_count), 2)
        high_hot = (high[:, :, None] == targets).astype(jnp.bfloat16)
        counts = jnp.einsum("bwh,bwl->bhl", high_hot, low_hot, preferred_element_type=jnp.float32)
        counts = counts.astype(jnp.bfloat16).reshape(bag_count, block)
        piece = lax.dynamic_slice_in_dim(table, index * block, block, 0)
        return total + jnp.dot(counts, piece, preferred_element_type=jnp.float32)

    start = jnp.zeros((bag_count, table.shape[1]), jnp.float32)
    return lax.fori_loop(0, rows_dev // block, add_block, start)


def place_bags(values, lengths, samples, sample_count):
    scaled = values / jnp.sqrt(lengths.astype(jnp.float32))[:, :, None]
    slots = lax.broadcasted_iota(jnp.int32, samples.shape + (sample_count,), 2)
    picks = (samples[:, :, None] == slots).astype(jnp.float32)
    return jnp.sum(picks[:, :, :, None] * scaled[:, :, None, :], axis=0)


def on_device(emb, short_rows, short_len, short_sample, long_rows, long_len, long_sample):
    tab_dev = emb.shape[0]
    short_keys = mask_rows(short_rows, short_len)
    long_keys = mask_rows(long_rows, long_len)
    short_moved, long_moved = (
        lax.all_to_all(short_keys, "table", split_axis=1, concat_axis=0, tiled=True),
        lax.all_to_all(long_keys, "table", split_axis=1, concat_axis=0, tiled=True),
    )
    short_all, long_all = (
        lax.all_gather(short_moved, "batch", axis=0, tiled=True),
        lax.all_gather(long_moved, "batch", axis=0, tiled=True),
    )
    row_base = lax.axis_index("batch") * emb.shape[1]
    short_part = jnp.stack([pool_rows(short_all[:, 0, :], emb[0], row_base)], axis=1)
    long_part = jnp.stack([pool_rows(long_all[:, 0, :], emb[0], row_base)], axis=1)
    short_sum, long_sum = (
        lax.psum_scatter(short_part, "batch", scatter_dimension=0, tiled=True),
        lax.psum_scatter(long_part, "batch", scatter_dimension=0, tiled=True),
    )
    short_back, long_back = (
        lax.all_to_all(short_sum, "table", split_axis=0, concat_axis=1, tiled=True),
        lax.all_to_all(long_sum, "table", split_axis=0, concat_axis=1, tiled=True),
    )
    sample_count = short_sample.shape[0] + long_sample.shape[0]
    pooled = place_bags(short_back, short_len, short_sample, sample_count)
    pooled = pooled + place_bags(long_back, long_len, long_sample, sample_count)
    return jnp.transpose(pooled, (1, 0, 2))


def solution(mesh):
    return jax.shard_map(
        on_device,
        mesh=mesh,
        in_specs=(
            P("table", "batch", None),
            P(("table", "batch"), None, None),
            P(("table", "batch"), None),
            P(("table", "batch"), None),
            P(("table", "batch"), None, None),
            P(("table", "batch"), None),
            P(("table", "batch"), None),
        ),
        out_specs=P(("table", "batch"), None, None),
        check_vma=False,
    )
```

profile of v0, /device:TPU:0, one launch (start us, length us, event | category | flops | bytes accessed | tf_op | source)
XLA Modules:
  0.0 266.0 jit_solution(12417706467865206309)
XLA Ops:
  6.5 0.8 fusion.56
  7.3 0.7 reshape.94
  8.0 4.3 %all-to-all-start = ((s32[4,1,192]{2,1,0:T(1,128)}), s32[4,1,192]{2,1,0:T(1,128)S(1)}, u32[]{:S(2)}, u32[]{:S(2)}) async-start(s32[4,1,192]{2,1,0:T(1,128)} %reshape.94), calls=%async_computation | async-start | bytes 8192 | tf_op jit(solution)/shard_map/all_to_all | solution.py:49
  12.2 0.7 convert_sqrt_fusion
  12.9 0.8 copy.38
  13.8 0.8 copy.42
  14.6 0.7 fusion.55
  15.3 1.4 compare_select_fusion
  16.7 0.7 convert_sqrt_fusion.1
  17.4 0.1 copy.45
  17.5 1.3 dynamic-slice
  19.4 3.3 %all-to-all-start.2 = ((s32[2,4,512]{2,0,1:T(2,128)}), s32[2,4,512]{2,0,1:T(2,128)S(1)}, u32[]{:S(2)}, u32[]{:S(2)}) async-start(s32[2,4,512]{2,0,1:T(2,128)} %compare_select_fusion), calls=%async_computation.2 | async-start | bytes 32768 | tf_op jit(solution)/shard_map/all_to_all | solution.py:50
  22.7 0.5 broadcast.136
  23.2 0.7 reduce
  23.9 0.1 reshape.95
  24.0 31.3 %all_gather.6 = s32[192,1,32]{2,1,0:T(1,128)S(1)} all-gather(s32[24,1,32]{2,1,0:T(1,128)S(1)} %all_to_all.51), channel_id=1, replica_groups=mesh['table'=4,'batch'=8] {'batch'}, dimensions={0}, use_global_device_ids=true | all-gather | bytes 27648 | tf_op jit(solution)/shard_map/all_gather | solution.py:53
  55.3 0.1 fusion.50
  55.4 30.5 %all_gather.7 = s32[64,1,512]{2,0,1:T(8,128)S(1)} all-gather(s32[8,1,512]{2,0,1:T(8,128)S(1)} %all_to_all.58), channel_id=1, replica_groups=mesh['table'=4,'batch'=8] {'batch'}, dimensions={0}, use_global_device_ids=true | all-gather | bytes 147456 | tf_op jit(solution)/shard_map/all_gather | solution.py:54
  85.9 0.1 fusion.45
  86.1 31.9 %while.29 = (s32[]{:T(128)}, f32[64,128]{1,0:T(8,128)S(1)}, s32[64,512]{1,0:T(8,128)S(1)}, bf16[32768,128]{1,0:T(8,128)(2,1)}, s32[64,512]{1,0:T(8,128)S(1)}, /*...) while((s32[]{:T(128)}, f32[64,128]{1,0:T(8,128)S(1)}, s32[64,512]{1,0:T(8,128)S(1)}, ...), condition=%wide.region_5.6_spmd.clone, body=%wide.region_4.5_spmd.clone.sunk | while | flops 682115136 | bytes 4522681 | solution.py:34
  86.1 5.5 %fusion.79 = bf16[64,64,128]{2,1,0:T(8,128)(2,1)S(1)} fusion(s32[64,512]{1,0:T(8,128)S(1)} %get-tuple-element.377, s32[64,512]{1,0:T(8,128)S(1)} %get-tuple-element.375, s32[64]{0:T(128)S(1)} %iota_add_fusion.5), kind=kOutput, calls=%fused_computation.26.clone.1 | convolution fusion | flops 547880960 | bytes 1310976 | tf_op jit(solution)/shard_map/while/body/eval_jaxpr/bwh,bwl->bhl/dot_general | solution.py:28
  91.6 2.4 fusion.80
  94.1 5.5 %fusion.79 = bf16[64,64,128]{2,1,0:T(8,128)(2,1)S(1)} fusion(s32[64,512]{1,0:T(8,128)S(1)} %get-tuple-element.377, s32[64,512]{1,0:T(8,128)S(1)} %get-tuple-element.375, s32[64]{0:T(128)S(1)} %iota_add_fusion.5), kind=kOutput, calls=%fused_computation.26.clone.1 | convolution fusion | flops 547880960 | bytes 1310976 | tf_op jit(solution)/shard_map/while/body/eval_jaxpr/bwh,bwl->bhl/dot_general | solution.py:28
  99.6 2.4 fusion.80
  102.1 5.5 %fusion.79 = bf16[64,64,128]{2,1,0:T(8,128)(2,1)S(1)} fusion(s32[64,512]{1,0:T(8,128)S(1)} %get-tuple-element.377, s32[64,512]{1,0:T(8,128)S(1)} %get-tuple-element.375, s32[64]{0:T(128)S(1)} %iota_add_fusion.5), kind=kOutput, calls=%fused_computation.26.clone.1 | convolution fusion | flops 547880960 | bytes 1310976 | tf_op jit(solution)/shard_map/while/body/eval_jaxpr/bwh,bwl->bhl/dot_general | solution.py:28
  107.6 2.4 fusion.80
  110.1 5.5 %fusion.79 = bf16[64,64,128]{2,1,0:T(8,128)(2,1)S(1)} fusion(s32[64,512]{1,0:T(8,128)S(1)} %get-tuple-element.377, s32[64,512]{1,0:T(8,128)S(1)} %get-tuple-element.375, s32[64]{0:T(128)S(1)} %iota_add_fusion.5), kind=kOutput, calls=%fused_computation.26.clone.1 | convolution fusion | flops 547880960 | bytes 1310976 | tf_op jit(solution)/shard_map/while/body/eval_jaxpr/bwh,bwl->bhl/dot_general | solution.py:28
  115.6 2.4 fusion.80
  118.0 37.0 %all-reduce.1 = f32[64,1,128]{2,0,1:T(8,128)S(1)} all-reduce(f32[64,1,128]{2,0,1:T(8,128)S(1)} %bitcast.97), channel_id=3, replica_groups=mesh['table'=4,'batch'=8] {'batch'}, use_global_device_ids=true, to_apply=%region_6.7.clone | all-reduce | flops 8192 | bytes 65536
  155.1 0.6 constant_dynamic-slice_fusion
  155.7 3.3 %all-to-all-start.3 = ((f32[8,1,128]{2,1,0:T(1,128)}), f32[8,1,128]{2,1,0:T(1,128)S(1)}, u32[]{:S(2)}, u32[]{:S(2)}) async-start(f32[8,1,128]{2,1,0:T(1,128)} %bitcast.13), calls=%async_computation.3 | async-start | bytes 8192 | tf_op jit(solution)/shard_map/all_to_all | solution.py:65
  159.0 35.0 %while.28 = (s32[]{:T(128)}, f32[192,128]{1,0:T(8,128)S(1)}, s32[192,32]{1,0:T(8,128)S(1)}, bf16[32768,128]{1,0:T(8,128)(2,1)}, s32[192,32]{1,0:T(8,128)S(1)}, /...) while((s32[]{:T(128)}, f32[192,128]{1,0:T(8,128)S(1)}, s32[192,32]{1,0:T(8,128)S(1)}, ...), condition=%wide.region_1.2_spmd.clone, body=%wide.region_0.1_spmd.clone.sunk | while | flops 506904640 | bytes 8635065 | solution.py:34
  159.0 5.1 %fusion.73 = bf16[192,64,128]{2,1,0:T(8,128)(2,1)S(1)} fusion(s32[192,32]{1,0:T(8,128)S(1)} %get-tuple-element.347, s32[64]{0:T(128)S(1)} %iota_add_fusion.4, s32[192,32]{1,0:T(8,128)S(1)} %get-tuple-element.345), kind=kOutput, calls=%fused_computation.9.clone.1 | convolution fusion | flops 104202240 | bytes 3195136 | tf_op jit(solution)/shard_map/while/body/eval_jaxpr/bwh,bwl->bhl/dot_general | solution.py:28
  164.1 3.6 %fusion.74 = f32[192,128]{1,0:T(8,128)S(1)} fusion(bf16[32768,128]{1,0:T(8,128)(2,1)} %get-tuple-element.346, s32[]{:T(128)S(6)} %select_n.109, bf16[24,8,64,128]{3,2,1,0:T(8,128)(2,1)S(1)} %bitcast.106, f32[192,128]{1,0:T(8,128)S(1)} %get-tuple-element.334, pred[]{:T(512)S(6)} %compare.18), kind=kOutput, calls=%fused_computation.14.clone.1 | convolution fusion | flops 402702336 | bytes 5439493 | tf_op jit(solution)/shard_map/while/body/eval_jaxpr/dot_general | solution.py:31
  167.7 5.1 %fusion.73 = bf16[192,64,128]{2,1,0:T(8,128)(2,1)S(1)} fusion(s32[192,32]{1,0:T(8,128)S(1)} %get-tuple-element.347, s32[64]{0:T(128)S(1)} %iota_add_fusion.4, s32[192,32]{1,0:T(8,128)S(1)} %get-tuple-element.345), kind=kOutput, calls=%fused_computation.9.clone.1 | convolution fusion | flops 104202240 | bytes 3195136 | tf_op jit(solution)/shard_map/while/body/eval_jaxpr/bwh,bwl->bhl/dot_general | solution.py:28
  172.8 3.6 %fusion.74 = f32[192,128]{1,0:T(8,128)S(1)} fusion(bf16[32768,128]{1,0:T(8,128)(2,1)} %get-tuple-element.346, s32[]{:T(128)S(6)} %select_n.109, bf16[24,8,64,128]{3,2,1,0:T(8,128)(2,1)S(1)} %bitcast.106, f32[192,128]{1,0:T(8,128)S(1)} %get-tuple-element.334, pred[]{:T(512)S(6)} %compare.18), kind=kOutput, calls=%fused_computation.14.clone.1 | convolution fusion | flops 402702336 | bytes 5439493 | tf_op jit(solution)/shard_map/while/body/eval_jaxpr/dot_general | solution.py:31
  176.5 5.1 %fusion.73 = bf16[192,64,128]{2,1,0:T(8,128)(2,1)S(1)} fusion(s32[192,32]{1,0:T(8,128)S(1)} %get-tuple-element.347, s32[64]{0:T(128)S(1)} %iota_add_fusion.4, s32[192,32]{1,0:T(8,128)S(1)} %get-tuple-element.345), kind=kOutput, calls=%fused_computation.9.clone.1 | convolution fusion | flops 104202240 | bytes 3195136 | tf_op jit(solution)/shard_map/while/body/eval_jaxpr/bwh,bwl->bhl/dot_general | solution.py:28
  181.6 3.6 %fusion.74 = f32[192,128]{1,0:T(8,128)S(1)} fusion(bf16[32768,128]{1,0:T(8,128)(2,1)} %get-tuple-element.346, s32[]{:T(128)S(6)} %select_n.109, bf16[24,8,64,128]{3,2,1,0:T(8,128)(2,1)S(1)} %bitcast.106, f32[192,128]{1,0:T(8,128)S(1)} %get-tuple-element.334, pred[]{:T(512)S(6)} %compare.18), kind=kOutput, calls=%fused_computation.14.clone.1 | convolution fusion | flops 402702336 | bytes 5439493 | tf_op jit(solution)/shard_map/while/body/eval_jaxpr/dot_general | solution.py:31
  185.2 5.1 %fusion.73 = bf16[192,64,128]{2,1,0:T(8,128)(2,1)S(1)} fusion(s32[192,32]{1,0:T(8,128)S(1)} %get-tuple-element.347, s32[64]{0:T(128)S(1)} %iota_add_fusion.4, s32[192,32]{1,0:T(8,128)S(1)} %get-tuple-element.345), kind=kOutput, calls=%fused_computation.9.clone.1 | convolution fusion | flops 104202240 | bytes 3195136 | tf_op jit(solution)/shard_map/while/body/eval_jaxpr/bwh,bwl->bhl/dot_general | solution.py:28
  190.3 3.6 %fusion.74 = f32[192,128]{1,0:T(8,128)S(1)} fusion(bf16[32768,128]{1,0:T(8,128)(2,1)} %get-tuple-element.346, s32[]{:T(128)S(6)} %select_n.109, bf16[24,8,64,128]{3,2,1,0:T(8,128)(2,1)S(1)} %bitcast.106, f32[192,128]{1,0:T(8,128)S(1)} %get-tuple-element.334, pred[]{:T(512)S(6)} %compare.18), kind=kOutput, calls=%fused_computation.14.clone.1 | convolution fusion | flops 402702336 | bytes 5439493 | tf_op jit(solution)/shard_map/while/body/eval_jaxpr/dot_general | solution.py:31
  194.0 0.6 copy-done
  194.6 0.1 divide_bitcast_fusion
  194.7 56.6 %reduce-scatter.6.cloned.1.call-done = f32[24,1,128]{2,0,1:T(8,128)} async-done(((f32[192,1,128]{2,0,1:T(8,128)}), f32[24,1,128]{2,0,1:T(8,128)}) %reduce-scatter.6.cloned.1.call-update) | async-done | bytes 12304
  251.3 3.2 %all-to-all-start.1 = ((f32[24,1,128]{2,1,0:T(1,128)}), f32[24,1,128]{2,1,0:T(1,128)S(1)}, u32[]{:S(2)}, u32[]{:S(2)}) async-start(f32[24,1,128]{2,1,0:T(1,128)} %bitcast.105), calls=%async_computation.1 | async-start | bytes 24576 | tf_op jit(solution)/shard_map/all_to_all | solution.py:64
  254.6 3.7 %all-to-all-done.1 = f32[24,1,128]{2,1,0:T(1,128)S(1)} async-done(((f32[24,1,128]{2,1,0:T(1,128)}), f32[24,1,128]{2,1,0:T(1,128)S(1)}, u32[]{:S(2)}, u32[]{:S(2)}) %all-to-all-start.1) | async-done | bytes 12320 | tf_op jit(solution)/shard_map/all_to_all | solution.py:64
  258.3 0.1 broadcast_divide_fusion
  258.4 0.1 multiply_reduce_fusion
  258.6 0.6 copy.47
  (25 shorter events, 0.3 us)
Async XLA Ops:
  8.0 11.4 %all-to-all-start = ((s32[4,1,192]{2,1,0:T(1,128)}), s32[4,1,192]{2,1,0:T(1,128)S(1)}, u32[]{:S(2)}, u32[]{:S(2)}) async-start(s32[4,1,192]{2,1,0:T(1,128)} %reshape.94), calls=%async_computation | async-start | bytes 8192 | tf_op jit(solution)/shard_map/all_to_all | solution.py:49
  19.4 36.0 %all-to-all-start.2 = ((s32[2,4,512]{2,0,1:T(2,128)}), s32[2,4,512]{2,0,1:T(2,128)S(1)}, u32[]{:S(2)}, u32[]{:S(2)}) async-start(s32[2,4,512]{2,0,1:T(2,128)} %compare_select_fusion), calls=%async_computation.2 | async-start | bytes 32768 | tf_op jit(solution)/shard_map/all_to_all | solution.py:50
  155.7 39.0 %all-to-all-start.3 = ((f32[8,1,128]{2,1,0:T(1,128)}), f32[8,1,128]{2,1,0:T(1,128)S(1)}, u32[]{:S(2)}, u32[]{:S(2)}) async-start(f32[8,1,128]{2,1,0:T(1,128)} %bitcast.13), calls=%async_computation.3 | async-start | bytes 8192 | tf_op jit(solution)/shard_map/all_to_all | solution.py:65
  158.9 92.3 %reduce-scatter.6.cloned.1.call-start = ((), (), s32[]{:S(2)}) async-start(), calls=%async_computation.5 | async-start | bytes 110592
  194.0 0.6 copy-start
  251.3 7.0 %all-to-all-start.1 = ((f32[24,1,128]{2,1,0:T(1,128)}), f32[24,1,128]{2,1,0:T(1,128)S(1)}, u32[]{:S(2)}, u32[]{:S(2)}) async-start(f32[24,1,128]{2,1,0:T(1,128)} %bitcast.105), calls=%async_computation.1 | async-start | bytes 24576 | tf_op jit(solution)/shard_map/all_to_all | solution.py:64
Sparse Core Ops, SparseCore 0:
  194.7 56.4 reduce-scatter.5
where the time goes:
time: 267 us; the launch traced here: 266 us
  blocking collectives  98.9 us (37%)
  matrix products  66.5 us (25%)
  waiting for transfers between devices  60.3 us (23%)
  starting transfers between devices  14.1 us (5%)
  between operations  14.1 us (5%)
  local copies, waits for them, and re-layouts  6.04 us (2%)
  other arithmetic  5.64 us (2%)
    unnamed x2, waiting for transfers between devices  56.6 us
    dot_general x8, matrix products, add_block(): jnp.einsum('bwh,bwl->bhl', high_hot, low_hot, preferred_element_type=jnp....  42.2 us
    unnamed x1, blocking collectives  37 us
    all_gather x1, blocking collectives, on_device(): lax.all_gather(short_moved, 'batch', axis=0, tiled=True)  31.3 us
    all_gather x1, blocking collectives, on_device(): lax.all_gather(long_moved, 'batch', axis=0, tiled=True)  30.5 us
    dot_general x8, matrix products, add_block(): return total + jnp.dot(counts, piece, preferred_element_type=jnp.float32)  24.3 us
  transfers between devices with their start and end apart: 5, of which 2 were waited for; matrix products, arithmetic and copies ran while one was open for 16% of the time, Pallas kernels for 0%

commit v1 on v0

v1 whole, which is shorter than its diff:
```python
import functools

import jax
import jax.numpy as jnp
from jax import lax
from jax.experimental import pallas as pl
from jax.experimental.pallas import tpu as pltpu
from jax.sharding import PartitionSpec as P

LOW = 256
LANES = 128
SUB = 8


def pool_kernel(base_ref, ids_ref, table_hbm, out_ref, table_ref, key_ref, low_ref, counts_ref, sem,
                *, senders, slots, short_bags, width, long_bags, long_width, pitch):
    rows_dev = table_ref.shape[0]
    highs = rows_dev // LOW
    short_span = slots * width
    half = highs * pitch

    load = pltpu.make_async_copy(table_hbm, table_ref, sem)

    @pl.when(pl.program_id(0) == 0)
    def _():
        load.start()

    local = ids_ref[...] - base_ref[0]
    inside = (local >= 0) & (local < rows_dev)
    high = local // LOW
    place = lax.broadcasted_iota(jnp.int32, local.shape, 1)
    key = jnp.where(place < short_span, high * slots + place // width, high)
    key_ref[...] = jnp.where(inside, key, -1)
    low_ref[...] = local % LOW

    def hot(values, count):
        size = values.shape[1]
        spot = lax.broadcasted_iota(jnp.int32, (count, size), 0)
        return (spot == values).astype(jnp.float32).astype(jnp.bfloat16)

    def tally(key, low, count):
        return lax.dot_general(hot(key, count), hot(low, LOW), (((1,), (1,)), ((), ())),
                               preferred_element_type=jnp.float32)

    def count_sender(s, carry):
        span = pl.ds(0, short_span)
        res = tally(key_ref[pl.ds(s, 1), span], low_ref[pl.ds(s, 1), span], highs * slots)
        for part in range(LOW // LANES):
            piece = res[:, part * LANES:(part + 1) * LANES]
            for h in range(highs):
                row = pl.multiple_of(part * half + h * pitch + s * slots, SUB)
                counts_ref[pl.ds(row, slots), :] = piece[h * slots:(h + 1) * slots, :]
        for bag in range(long_bags):
            span = pl.ds(short_span + bag * long_width, long_width)
            res = tally(key_ref[pl.ds(s, 1), span], low_ref[pl.ds(s, 1), span], highs)
            for part in range(LOW // LANES):
                row = part * half + s * slots + short_bags + bag
                counts_ref[pl.ds(row, highs, stride=pitch), :] = res[:, part * LANES:(part + 1) * LANES]
        return carry

    lax.fori_loop(0, senders, count_sender, 0)

    @pl.when(pl.program_id(0) == 0)
    def _():
        load.wait()

    bags = senders * slots
    step = 4 if highs % 4 == 0 else 1

    def add_rows(index, total):
        pieces = []
        for k in range(step):
            h = index * step + k
            for part in range(LOW // LANES):
                row = pl.multiple_of(part * half + h * pitch, SUB)
                pieces.append(counts_ref[pl.ds(row, bags), :].astype(jnp.bfloat16))
        lhs = jnp.concatenate(pieces, axis=1)
        rhs = table_ref[pl.ds(pl.multiple_of(index * step * LOW, LOW), step * LOW), :]
        return total + jnp.dot(lhs, rhs, preferred_element_type=jnp.float32)

    out_ref[...] = lax.fori_loop(0, highs // step, add_rows, jnp.zeros(out_ref.shape, jnp.float32))


def pool(ids, table, row_base, slots, short_bags, width, long_bags, long_width):
    count, span = ids.shape
    senders = min(32, count)
    rows_dev, dim = table.shape
    highs = rows_dev // LOW
    bags = senders * slots
    pitch = bags + SUB
    body = functools.partial(pool_kernel, senders=senders, slots=slots, short_bags=short_bags, width=width,
                             long_bags=long_bags, long_width=long_width, pitch=pitch)
    return pl.pallas_call(
        body,
        out_shape=jax.ShapeDtypeStruct((count * slots, dim), jnp.float32),
        grid=(count // senders,),
        in_specs=[
            pl.BlockSpec(memory_space=pltpu.SMEM),
            pl.BlockSpec((senders, span), lambda i: (i, 0)),
            pl.BlockSpec(memory_space=pl.ANY),
        ],
        out_specs=pl.BlockSpec((bags, dim), lambda i: (i, 0)),
        scratch_shapes=[
            pltpu.VMEM((rows_dev, dim), table.dtype),
            pltpu.VMEM((senders, span), jnp.int32),
            pltpu.VMEM((senders, span), jnp.int32),
            pltpu.VMEM((LOW // LANES * highs * pitch, LANES), jnp.float32),
            pltpu.SemaphoreType.DMA,
        ],
        compiler_params=pltpu.CompilerParams(
            dimension_semantics=("arbitrary",), vmem_limit_bytes=56 * 2**20),
        name="pool",
    )(row_base, ids, table)


def place_kernel(got_ref, weight_ref, out_ref, *, tables, batch):
    for t in range(tables):
        total = got_ref[t * batch]
        for b in range(1, batch):
            total = total + got_ref[t * batch + b]
        weight = weight_ref[t]
        placed = weight[:, 0:1] * total[0:1, :]
        for j in range(1, total.shape[0]):
            placed = placed + weight[:, j:j + 1] * total[j:j + 1, :]
        out_ref[:, t, :] = placed


def place(got, weight, tables, batch):
    slots, dim = got.shape[1:]
    return pl.pallas_call(
        functools.partial(place_kernel, tables=tables, batch=batch),
        out_shape=jax.ShapeDtypeStruct((slots, tables, dim), jnp.float32),
        name="place",
    )(got, weight)


def mask_rows(rows, lengths):
    spot = lax.broadcasted_iota(jnp.int32, rows.shape, 2)
    return jnp.where(spot < lengths[:, :, None], rows, -1)


def make_on_device(axes, tables, batch):
    devices = tables * batch

    def on_device(emb, short_rows, short_len, short_sample, long_rows, long_len, long_sample):
        short_bags, _, width = short_rows.shape
        long_bags, _, long_width = long_rows.shape
        slots = short_bags + long_bags
        short_keys = mask_rows(short_rows, short_len)
        short_keys = jnp.pad(short_keys, ((0, long_bags), (0, 0), (0, 0)), constant_values=-1)
        long_keys = mask_rows(long_rows, long_len)
        keys = jnp.concatenate(
            [jnp.transpose(short_keys, (1, 0, 2)).reshape(tables, slots * width),
             jnp.transpose(long_keys, (1, 0, 2)).reshape(tables, long_bags * long_width)], axis=1)
        span = keys.shape[1]
        sent = jnp.broadcast_to(keys[:, None, :], (tables, batch, span)).reshape(devices, span)
        ids = lax.all_to_all(sent, axes, split_axis=0, concat_axis=0, tiled=True)
        row_base = (lax.axis_index(axes[1]) * emb.shape[1]).astype(jnp.int32).reshape(1)
        part = pool(ids, emb[0], row_base, slots, short_bags, width, long_bags, long_width)
        got = lax.all_to_all(part.reshape(devices, slots, part.shape[1]), axes,
                             split_axis=0, concat_axis=0, tiled=True)
        sample = jnp.concatenate([short_sample, long_sample], axis=0)
        length = jnp.concatenate([short_len, long_len], axis=0).astype(jnp.float32)
        spot = lax.broadcasted_iota(jnp.int32, (tables, slots, slots), 1)
        weight = jnp.where(spot == sample.T[:, None, :], 1.0 / jnp.sqrt(length.T)[:, None, :], 0.0)
        return place(got, weight, tables, batch)

    return on_device


def solution(mesh):
    axes = ("table", "batch")
    return jax.shard_map(
        make_on_device(axes, mesh.shape["table"], mesh.shape["batch"]),
        mesh=mesh,
        in_specs=(
            P("table", "batch", None),
            P(("table", "batch"), None, None),
            P(("table", "batch"), None),
            P(("table", "batch"), None),
            P(("table", "batch"), None, None),
            P(("table", "batch"), None),
            P(("table", "batch"), None),
        ),
        out_specs=P(("table", "batch"), None, None),
        check_vma=False,
    )
```

time: 267 us -> 59.6 us (0.22)
  blocking collectives: 98.9 us -> 0 us
  matrix products: 66.5 us -> 0 us
  waiting for transfers between devices: 60.3 us -> 12.8 us
  Pallas kernels: 0 us -> 28.4 us
  between operations: 14.1 us -> 0.06 us
  starting transfers between devices: 14.1 us -> 10.2 us
    dot_general x16 -> x0, matrix products: 66.5 us -> none  [the longest x8 42.2 us: add_block(): jnp.einsum('bwh,bwl->bhl', high_hot, low_hot, preferred_element_type=jnp....]
    all_gather x2 -> x0, blocking collectives: 61.8 us -> none  [the longest x1 31.3 us: on_device(): lax.all_gather(short_moved, 'batch', axis=0, tiled=True)]
    unnamed x2 -> x0, waiting for transfers between devices: 56.6 us -> none
    unnamed x1 -> x0, blocking collectives: 37 us -> none
    pallas_call x0 -> x2, Pallas kernels: none -> 28.4 us  [the longest x1 26.8 us: pool(): pl.pallas_call(body, out_shape=jax.ShapeDtypeStruct((count * slots, dim),...]
    all_to_all x4 -> x2, waiting for transfers between devices: 3.73 us -> 12.8 us  [the longest x1 7.11 us: on_device(): lax.all_to_all(part.reshape(devices, slots, part.shape[1]), axes, split_a...]
    all_to_all x4 -> x2, starting transfers between devices: 14.1 us -> 10.2 us  [the longest x1 7.33 us: on_device(): ids = lax.all_to_all(sent, axes, split_axis=0, concat_axis=0, tiled=True)]
  transfers between devices with their start and end apart: 5 -> 2, of which waited for: 2 -> 2; matrix products, arithmetic and copies ran while one was open for 16% -> 5% of each run, Pallas kernels for 0% -> 0%
where the time goes in v1:
time: 59.6 us; the launch traced here: 59.1 us
  Pallas kernels  28.4 us (48%)
  waiting for transfers between devices  12.8 us (21%)
  starting transfers between devices  10.2 us (17%)
  local copies, waits for them, and re-layouts  4.57 us (8%)
  other arithmetic  3.02 us (5%)
    pallas_call x1, Pallas kernels, pool(): pl.pallas_call(body, out_shape=jax.ShapeDtypeStruct((count * slots, dim),...  26.8 us
    all_to_all x1, starting transfers between devices, on_device(): ids = lax.all_to_all(sent, axes, split_axis=0, concat_axis=0, tiled=True)  7.33 us
    all_to_all x1, waiting for transfers between devices, on_device(): lax.all_to_all(part.reshape(devices, slots, part.shape[1]), axes, split_a...  7.11 us
    all_to_all x1, waiting for transfers between devices, on_device(): ids = lax.all_to_all(sent, axes, split_axis=0, concat_axis=0, tiled=True)  5.72 us
    unnamed x8, local copies, waits for them, and re-layouts  3.63 us
    all_to_all x1, starting transfers between devices, on_device(): lax.all_to_all(part.reshape(devices, slots, part.shape[1]), axes, split_a...  2.87 us
    pallas_call x1, Pallas kernels, place(): pl.pallas_call(functools.partial(place_kernel, tables=tables, batch=batch...  1.64 us
    select_n x2, other arithmetic, mask_rows(): return jnp.where(spot < lengths[:, :, None], rows, -1)  1.57 us
  transfers between devices with their start and end apart: 2, of which 2 were waited for; matrix products, arithmetic and copies ran while one was open for 5% of the time, Pallas kernels for 0%

profile of v1, /device:TPU:0, one launch (start us, length us, event | category | flops | bytes accessed | tf_op | source)
XLA Modules:
  0.0 59.1 jit_solution(3839842728177551471)
XLA Ops:
  0.0 0.0 copy-start.1
  0.0 0.8 %copy.15 = s32[6,4]{1,0:T(8,128)S(1)} copy(s32[6,4]{0,1:T(4,128)} %param.9) | data formatting | bytes 192 | tf_op args[2]
  0.8 0.8 %fusion.2 = s32[6,4,32]{2,1,0:T(4,128)S(1)} fusion(s32[6,4,32]{2,1,0:T(4,128)} %param.8, s32[6,4]{1,0:T(8,128)S(1)} %copy.15), kind=kLoop, calls=%fused_computation.8 | loop fusion | flops 1536 | bytes 6240 | tf_op jit(solution)/shard_map/jit(_where)/select_n | solution.py:139
  1.6 0.1 reshape.23
  1.7 0.8 %fusion = s32[2,4,512]{2,1,0:T(4,128)S(1)} fusion(s32[2,4,512]{2,1,0:T(4,128)} %param.11, s32[2,4]{1,0:T(2,128)} %param.12), kind=kLoop, calls=%fused_computation.5 | loop fusion | flops 8192 | bytes 32800 | tf_op jit(solution)/shard_map/jit(_where)/select_n | solution.py:139
  2.5 0.8 %all_to_all.10 = s32[32,1,1280]{2,1,0:T(1,128)} reshape(s32[4,8,1280]{2,1,0:T(8,128)S(1)} %broadcast_in_dim.32) | data formatting | bytes 327680 | tf_op jit(solution)/shard_map/all_to_all | solution.py:157
  3.3 7.3 %all-to-all-start = ((s32[32,1,1280]{2,1,0:T(1,128)}), s32[32,1,1280]{2,1,0:T(1,128)S(1)}, u32[]{:S(2)}, u32[]{:S(2)}) async-start(s32[32,1,1280]{2,1,0:T(1,128)} %all_to_all.10), calls=%async_computation | async-start | bytes 327680 | tf_op jit(solution)/shard_map/all_to_all | solution.py:157
  10.6 0.8 %copy.18 = s32[2,4]{0,1:T(4,128)S(1)} copy(s32[2,4]{1,0:T(2,128)} %param.12) | data formatting | bytes 64 | tf_op args[5]
  11.4 0.8 %copy.17 = s32[2,4]{0,1:T(4,128)S(1)} copy(s32[2,4]{1,0:T(2,128)} %param.13) | data formatting | bytes 64 | tf_op args[6]
  12.2 0.8 %fusion.4 = f32[4,8]{1,0:T(4,128)S(1)} fusion(s32[2,4]{0,1:T(4,128)S(1)} %copy.18, s32[6,4]{0,1:T(4,128)} %param.9), kind=kLoop, calls=%fused_computation.12 | loop fusion | flops 64 | bytes 256 | tf_op jit(solution)/shard_map/sqrt | solution.py:165
  12.9 5.7 %all-to-all-done = s32[32,1,1280]{2,1,0:T(1,128)S(1)} async-done(((s32[32,1,1280]{2,1,0:T(1,128)}), s32[32,1,1280]{2,1,0:T(1,128)S(1)}, u32[]{:S(2)}, u32[]{:S(2)}) %all-to-all-start) | async-done | bytes 163872 | tf_op jit(solution)/shard_map/all_to_all | solution.py:157
  18.7 0.7 %copy.21 = s32[32,1,1280]{2,0,1:T(8,128)} copy(s32[32,1,1280]{2,1,0:T(1,128)S(1)} %all-to-all-done) | data formatting | bytes 327680
  19.3 26.8 %pool.1 = f32[256,128]{1,0:T(8,128)} custom-call(s32[1]{0:T(128)} %bitcast.base_ref, s32[32,1280]{1,0:T(8,128)} %bitcast.16, bf16[32768,128]{1,0:T(8,128)(2,1)} %bitcast.15), custom_call_target="tpu_custom_call" | custom-call | tf_op jit(solution)/shard_map/pool/pallas_call | solution.py:93
  46.1 2.9 %all-to-all-start.1 = ((f32[32,8,128]{2,1,0:T(8,128)}), f32[32,8,128]{2,1,0:T(8,128)S(1)}, u32[]{:S(2)}, u32[]{:S(2)}) async-start(f32[32,8,128]{2,1,0:T(8,128)} %bitcast.17), calls=%async_computation.1 | async-start | bytes 262144 | tf_op jit(solution)/shard_map/all_to_all | solution.py:160
  49.0 0.0 copy-done.1
  49.0 0.1 add_bitcast_fusion
  49.1 0.6 %fusion.1.weight_ref = f32[4,8,8]{2,1,0:T(8,128)} fusion(f32[4,8]{1,0:T(4,128)S(1)} %fusion.4, s32[4,8]{1,0:T(4,128)S(1)} %add_bitcast_fusion), kind=kLoop, calls=%fused_computation.6 | loop fusion | flops 512 | bytes 1280 | tf_op jit(solution)/shard_map/jit(_where)/select_n | solution.py:165
  49.7 7.1 %all-to-all-done.1.got_ref = f32[32,8,128]{2,1,0:T(8,128)S(1)} async-done(((f32[32,8,128]{2,1,0:T(8,128)}), f32[32,8,128]{2,1,0:T(8,128)S(1)}, u32[]{:S(2)}, u32[]{:S(2)}) %all-to-all-start.1) | async-done | bytes 131104 | tf_op jit(solution)/shard_map/all_to_all | solution.py:160
  56.8 0.0 copy-start
  56.8 0.6 %copy-done = f32[32,8,128]{2,1,0:T(8,128)} copy-done((f32[32,8,128]{2,1,0:T(8,128)}, f32[32,8,128]{2,1,0:T(8,128)S(1)}, u32[]{:S(2)}) %copy-start) | copy-done | bytes 131096
  57.5 1.6 %place.1 = f32[8,4,128]{2,1,0:T(4,128)} custom-call(f32[32,8,128]{2,1,0:T(8,128)} %copy-done, f32[4,8,8]{2,1,0:T(8,128)} %fusion.1.weight_ref), custom_call_target="tpu_custom_call" | custom-call | tf_op jit(solution)/shard_map/place/pallas_call | solution.py:130
  (4 shorter events, 0.0 us)
Async XLA Ops:
  0.0 49.0 %copy-start.1 = (s32[6,4]{0,1:T(4,128)S(1)}, s32[6,4]{0,1:T(4,128)}, u32[]{:S(2)}) copy-start(s32[6,4]{0,1:T(4,128)} %param.10) | copy-start | bytes 292
  3.3 15.3 %all-to-all-start = ((s32[32,1,1280]{2,1,0:T(1,128)}), s32[32,1,1280]{2,1,0:T(1,128)S(1)}, u32[]{:S(2)}, u32[]{:S(2)}) async-start(s32[32,1,1280]{2,1,0:T(1,128)} %all_to_all.10), calls=%async_computation | async-start | bytes 327680 | tf_op jit(solution)/shard_map/all_to_all | solution.py:157
  46.1 10.7 %all-to-all-start.1 = ((f32[32,8,128]{2,1,0:T(8,128)}), f32[32,8,128]{2,1,0:T(8,128)S(1)}, u32[]{:S(2)}, u32[]{:S(2)}) async-start(f32[32,8,128]{2,1,0:T(8,128)} %bitcast.17), calls=%async_computation.1 | async-start | bytes 262144 | tf_op jit(solution)/shard_map/all_to_all | solution.py:160
  56.8 0.6 %copy-start = (f32[32,8,128]{2,1,0:T(8,128)}, f32[32,8,128]{2,1,0:T(8,128)S(1)}, u32[]{:S(2)}) copy-start(f32[32,8,128]{2,1,0:T(8,128)S(1)} %all-to-all-done.1.got_ref) | copy-start | bytes 393220

commit v2 on v1

--- a/solution.py
+++ b/solution.py
@@ -10,62 +10,85 @@
 LOW = 256
 LANES = 128
 SUB = 8
-
-
-def pool_kernel(base_ref, ids_ref, table_hbm, out_ref, table_ref, key_ref, low_ref, counts_ref, sem,
+PACK = 16
+UNROLL = 4
+LOW_BITS = 8
+HOT = jnp.float8_e4m3fn
+
+
+def pool_kernel(base_ref, ids_ref, table_hbm, out_ref, table_ref, counts_ref, sem,
                 *, senders, slots, short_bags, width, long_bags, long_width, pitch):
     rows_dev = table_ref.shape[0]
     highs = rows_dev // LOW
     short_span = slots * width
     half = highs * pitch
+    group = pl.program_id(0)
 
     load = pltpu.make_async_copy(table_hbm, table_ref, sem)
 
-    @pl.when(pl.program_id(0) == 0)
+    @pl.when(group == 0)
     def _():
         load.start()
 
-    local = ids_ref[...] - base_ref[0]
-    inside = (local >= 0) & (local < rows_dev)
-    high = local // LOW
-    place = lax.broadcasted_iota(jnp.int32, local.shape, 1)
-    key = jnp.where(place < short_span, high * slots + place // width, high)
-    key_ref[...] = jnp.where(inside, key, -1)
-    low_ref[...] = local % LOW
-
-    def hot(values, count):
-        size = values.shape[1]
-        spot = lax.broadcasted_iota(jnp.int32, (count, size), 0)
-        return (spot == values).astype(jnp.float32).astype(jnp.bfloat16)
-
-    def tally(key, low, count):
-        return lax.dot_general(hot(key, count), hot(low, LOW), (((1,), (1,)), ((), ())),
-                               preferred_element_type=jnp.float32)
+    one = jnp.ones((), jnp.bfloat16)
+    zero = jnp.zeros((), jnp.bfloat16)
+
+    def spread(values):
+        return jnp.broadcast_to(values, (PACK, values.shape[1]))
+
+    def hot(offsets, count, step):
+        offsets = offsets.astype(jnp.bfloat16)
+        blocks = [jnp.where(offsets == jnp.asarray(j * step, jnp.bfloat16), one, zero) for j in range(count)]
+        return jnp.concatenate(blocks, axis=0).astype(HOT)
+
+    def tally(left, right):
+        return lax.dot_general(left, right, (((1,), (1,)), ((), ())), preferred_element_type=jnp.float32)
 
     def count_sender(s, carry):
-        span = pl.ds(0, short_span)
-        res = tally(key_ref[pl.ds(s, 1), span], low_ref[pl.ds(s, 1), span], highs * slots)
+        local = ids_ref[group * senders + s] - base_ref[0]
+        inside = (local >= 0) & (local < rows_dev)
+        high = jnp.where(inside, local >> LOW_BITS, -64).astype(jnp.float32)
+        low = (local & (LOW - 1)).astype(jnp.float32)
+
+        def row_of(size):
+            return lax.broadcasted_iota(jnp.int32, (PACK, size), 0)
+
+        def low_hot(start, size):
+            return hot(spread(low[:, start:start + size]) - row_of(size).astype(jnp.float32), LOW // PACK, PACK)
+
+        row = row_of(short_span)
+        bag_of = lax.broadcasted_iota(jnp.int32, (PACK, short_span), 1) // width
+        per = PACK // slots
+        offsets = jnp.where(row % slots == bag_of,
+                            spread(high[:, :short_span]) - (row // slots).astype(jnp.float32), -64.0)
+        res = tally(hot(offsets, highs // per, per), low_hot(0, short_span))
         for part in range(LOW // LANES):
             piece = res[:, part * LANES:(part + 1) * LANES]
             for h in range(highs):
-                row = pl.multiple_of(part * half + h * pitch + s * slots, SUB)
-                counts_ref[pl.ds(row, slots), :] = piece[h * slots:(h + 1) * slots, :]
+                at = pl.multiple_of(part * half + h * pitch + s * slots, SUB)
+                counts_ref[pl.ds(at, slots), :] = piece[h * slots:(h + 1) * slots, :]
         for bag in range(long_bags):
-            span = pl.ds(short_span + bag * long_width, long_width)
-            res = tally(key_ref[pl.ds(s, 1), span], low_ref[pl.ds(s, 1), span], highs)
+            start = short_span + bag * long_width
+            offsets = spread(high[:, start:start + long_width]) - row_of(long_width).astype(jnp.float32)
+            res = tally(hot(offsets, highs // PACK, PACK), low_hot(start, long_width))
             for part in range(LOW // LANES):
-                row = part * half + s * slots + short_bags + bag
-                counts_ref[pl.ds(row, highs, stride=pitch), :] = res[:, part * LANES:(part + 1) * LANES]
+                at = part * half + s * slots + short_bags + bag
+                counts_ref[pl.ds(at, highs, stride=pitch), :] = res[:, part * LANES:(part + 1) * LANES]
         return carry
 
-    lax.fori_loop(0, senders, count_sender, 0)
-
-    @pl.when(pl.program_id(0) == 0)
+    def count_senders(index, carry):
+        for k in range(UNROLL):
+            count_sender(index * UNROLL + k, carry)
+        return carry
+
+    lax.fori_loop(0, senders // UNROLL, count_senders, 0)
+
+    @pl.when(group == 0)
     def _():
         load.wait()
 
     bags = senders * slots
-    step = 4 if highs % 4 == 0 else 1
+    step = 8 if highs % 8 == 0 else 1
 
     def add_rows(index, total):
         pieces = []
@@ -82,7 +105,7 @@
 
 
 def pool(ids, table, row_base, slots, short_bags, width, long_bags, long_width):
-    count, span = ids.shape
+    count, _, span = ids.shape
     senders = min(32, count)
     rows_dev, dim = table.shape
     highs = rows_dev // LOW
@@ -96,14 +119,12 @@
         grid=(count // senders,),
         in_specs=[
             pl.BlockSpec(memory_space=pltpu.SMEM),
-            pl.BlockSpec((senders, span), lambda i: (i, 0)),
+            pl.BlockSpec(memory_space=pltpu.VMEM),
             pl.BlockSpec(memory_space=pl.ANY),
         ],
         out_specs=pl.BlockSpec((bags, dim), lambda i: (i, 0)),
         scratch_shapes=[
             pltpu.VMEM((rows_dev, dim), table.dtype),
-            pltpu.VMEM((senders, span), jnp.int32),
-            pltpu.VMEM((senders, span), jnp.int32),
             pltpu.VMEM((LOW // LANES * highs * pitch, LANES), jnp.float32),
             pltpu.SemaphoreType.DMA,
         ],
@@ -130,13 +151,45 @@
     return pl.pallas_call(
         functools.partial(place_kernel, tables=tables, batch=batch),
         out_shape=jax.ShapeDtypeStruct((slots, tables, dim), jnp.float32),
+        in_specs=[pl.BlockSpec(memory_space=pltpu.VMEM), pl.BlockSpec(memory_space=pltpu.VMEM)],
+        out_specs=pl.BlockSpec(memory_space=pltpu.VMEM),
         name="place",
     )(got, weight)
 
 
-def mask_rows(rows, lengths):
-    spot = lax.broadcasted_iota(jnp.int32, rows.shape, 2)
-    return jnp.where(spot < lengths[:, :, None], rows, -1)
+def key_kernel(short_len_ref, long_len_ref, short_ref, long_ref, out_ref, *, batch):
+    short_bags, tables, width = short_ref.shape
+    long_bags, _, long_width = long_ref.shape
+    for t in range(tables):
+        pieces = []
+        for j in range(short_bags):
+            spot = lax.broadcasted_iota(jnp.int32, (1, width), 1)
+            pieces.append(jnp.where(spot < short_len_ref[t, j], short_ref[j, t:t + 1, :], -1))
+        pieces.append(jnp.full((1, long_bags * width), -1, jnp.int32))
+        for j in range(long_bags):
+            spot = lax.broadcasted_iota(jnp.int32, (1, long_width), 1)
+            pieces.append(jnp.where(spot < long_len_ref[j, t], long_ref[j, t:t + 1, :], -1))
+        row = jnp.concatenate(pieces, axis=1)
+        for b in range(batch):
+            out_ref[t * batch + b] = row
+
+
+def make_keys(short_rows, short_len, long_rows, long_len, batch):
+    short_bags, tables, width = short_rows.shape
+    long_bags, _, long_width = long_rows.shape
+    span = (short_bags + long_bags) * width + long_bags * long_width
+    return pl.pallas_call(
+        functools.partial(key_kernel, batch=batch),
+        out_shape=jax.ShapeDtypeStruct((tables * batch, 1, span), jnp.int32),
+        in_specs=[
+            pl.BlockSpec(memory_space=pltpu.SMEM),
+            pl.BlockSpec(memory_space=pltpu.SMEM),
+            pl.BlockSpec(memory_space=pltpu.VMEM),
+            pl.BlockSpec(memory_space=pltpu.VMEM),
+        ],
+        out_specs=pl.BlockSpec(memory_space=pltpu.VMEM),
+        name="keys",
+    )(short_len.T, long_len, short_rows, long_rows)
 
 
 def make_on_device(axes, tables, batch):
@@ -146,14 +199,7 @@
         short_bags, _, width = short_rows.shape
         long_bags, _, long_width = long_rows.shape
         slots = short_bags + long_bags
-        short_keys = mask_rows(short_rows, short_len)
-        short_keys = jnp.pad(short_keys, ((0, long_bags), (0, 0), (0, 0)), constant_values=-1)
-        long_keys = mask_rows(long_rows, long_len)
-        keys = jnp.concatenate(
-            [jnp.transpose(short_keys, (1, 0, 2)).reshape(tables, slots * width),
-             jnp.transpose(long_keys, (1, 0, 2)).reshape(tables, long_bags * long_width)], axis=1)
-        span = keys.shape[1]
-        sent = jnp.broadcast_to(keys[:, None, :], (tables, batch, span)).reshape(devices, span)
+        sent = make_keys(short_rows, short_len, long_rows, long_len, batch)
         ids = lax.all_to_all(sent, axes, split_axis=0, concat_axis=0, tiled=True)
         row_base = (lax.axis_index(axes[1]) * emb.shape[1]).astype(jnp.int32).reshape(1)
         part = pool(ids, emb[0], row_base, slots, short_bags, width, long_bags, long_width)

time: 59.6 us -> 47 us (0.79)
  Pallas kernels: 28.4 us -> 19.3 us
  local copies, waits for them, and re-layouts: 4.57 us -> 2.85 us
  other arithmetic: 3.02 us -> 1.44 us
    pallas_call x1, Pallas kernels: 26.8 us -> 16 us  [pool(): pl.pallas_call(body, out_shape=jax.ShapeDtypeStruct((count * slots, dim),...]
    pallas_call x0 -> x1, Pallas kernels: none -> 1.62 us  [make_keys(): pl.pallas_call(functools.partial(key_kernel, batch=batch), out_shape=jax....]
    select_n x2 -> x0, other arithmetic: 1.57 us -> none  [mask_rows(): return jnp.where(spot < lengths[:, :, None], rows, -1)]
    all_to_all x1 -> x0, local copies, waits for them, and re-layouts: 0.83 us -> none  [on_device(): ids = lax.all_to_all(sent, axes, split_axis=0, concat_axis=0, tiled=True)]
    unnamed x8, local copies, waits for them, and re-layouts: 3.63 us -> 2.85 us
  transfers between devices with their start and end apart: 2 -> 2, of which waited for: 2 -> 2; matrix products, arithmetic and copies ran while one was open for 5% -> 6% of each run, Pallas kernels for 0% -> 0%
where the time goes in v2:
time: 47 us; the launch traced here: 46.6 us
  Pallas kernels  19.3 us (41%)
  waiting for transfers between devices  12.8 us (27%)
  starting transfers between devices  10.2 us (22%)
  local copies, waits for them, and re-layouts  2.85 us (6%)
  other arithmetic  1.44 us (3%)
    pallas_call x1, Pallas kernels, pool(): pl.pallas_call(body, out_shape=jax.ShapeDtypeStruct((count * slots, dim),...  16 us
    all_to_all x1, starting transfers between devices, on_device(): ids = lax.all_to_all(sent, axes, split_axis=0, concat_axis=0, tiled=True)  7.33 us
    all_to_all x1, waiting for transfers between devices, on_device(): lax.all_to_all(part.reshape(devices, slots, part.shape[1]), axes, split_a...  7.12 us
    all_to_all x1, waiting for transfers between devices, on_device(): ids = lax.all_to_all(sent, axes, split_axis=0, concat_axis=0, tiled=True)  5.72 us
    all_to_all x1, starting transfers between devices, on_device(): lax.all_to_all(part.reshape(devices, slots, part.shape[1]), axes, split_a...  2.85 us
    unnamed x8, local copies, waits for them, and re-layouts  2.85 us
    pallas_call x1, Pallas kernels, place(): pl.pallas_call(functools.partial(place_kernel, tables=tables, batch=batch...  1.64 us
    pallas_call x1, Pallas kernels, make_keys(): pl.pallas_call(functools.partial(key_kernel, batch=batch), out_shape=jax....  1.62 us
  transfers between devices with their start and end apart: 2, of which 2 were waited for; matrix products, arithmetic and copies ran while one was open for 6% of the time, Pallas kernels for 0%

profile of v2, /device:TPU:0, one launch (start us, length us, event | category | flops | bytes accessed | tf_op | source)
XLA Modules:
  0.0 46.6 jit_solution(6470178576370853678)
XLA Ops:
  0.0 0.0 copy-start.2
  0.0 1.6 %keys.1 = s32[32,1,1280]{2,1,0:T(1,128)} custom-call(s32[4,6]{1,0:T(4,128)} %bitcast.10, s32[2,4]{1,0:T(2,128)} %long_len_ref.1, s32[6,4,32]{2,1,0:T(4,128)} %short_ref.1, s32[2,4,512]{2,1,0:T(4,128)} %long_ref.1), custom_call_target="tpu_custom_call" | custom-call | tf_op jit(solution)/shard_map/keys/pallas_call | solution.py:181
  1.6 7.3 %all-to-all-start = ((s32[32,1,1280]{2,1,0:T(1,128)}), s32[32,1,1280]{2,1,0:T(1,128)S(1)}, u32[]{:S(2)}, u32[]{:S(2)}) async-start(s32[32,1,1280]{2,1,0:T(1,128)} %keys.1), calls=%async_computation | async-start | bytes 327680 | tf_op jit(solution)/shard_map/all_to_all | solution.py:203
  9.0 0.8 %copy.9 = s32[2,4]{0,1:T(4,128)S(1)} copy(s32[2,4]{1,0:T(2,128)} %long_len_ref.1) | data formatting | bytes 64 | tf_op args[5]
  9.7 0.8 %copy.8 = s32[2,4]{0,1:T(4,128)S(1)} copy(s32[2,4]{1,0:T(2,128)} %param.13) | data formatting | bytes 64 | tf_op args[6]
  10.5 0.8 %fusion.2 = f32[4,8]{1,0:T(4,128)S(1)} fusion(s32[2,4]{0,1:T(4,128)S(1)} %copy.9, s32[6,4]{0,1:T(4,128)} %param.9), kind=kLoop, calls=%fused_computation.5 | loop fusion | flops 64 | bytes 256 | tf_op jit(solution)/shard_map/sqrt | solution.py:211
  11.3 5.7 %all-to-all-done.ids_ref = s32[32,1,1280]{2,1,0:T(1,128)S(1)} async-done(((s32[32,1,1280]{2,1,0:T(1,128)}), s32[32,1,1280]{2,1,0:T(1,128)S(1)}, u32[]{:S(2)}, u32[]{:S(2)}) %all-to-all-start) | async-done | bytes 163872 | tf_op jit(solution)/shard_map/all_to_all | solution.py:203
  17.0 0.0 copy-start
  17.0 0.7 %copy-done = s32[32,1,1280]{2,1,0:T(1,128)} copy-done((s32[32,1,1280]{2,1,0:T(1,128)}, s32[32,1,1280]{2,1,0:T(1,128)S(1)}, u32[]{:S(2)}) %copy-start) | copy-done | bytes 163864
  17.6 16.0 %pool.1 = f32[256,128]{1,0:T(8,128)} custom-call(s32[1]{0:T(128)} %bitcast.base_ref, s32[32,1,1280]{2,1,0:T(1,128)} %copy-done, bf16[32768,128]{1,0:T(8,128)(2,1)} %bitcast.8), custom_call_target="tpu_custom_call" | custom-call | tf_op jit(solution)/shard_map/pool/pallas_call | solution.py:116
  33.7 2.9 %all-to-all-start.1 = ((f32[32,8,128]{2,1,0:T(8,128)}), f32[32,8,128]{2,1,0:T(8,128)S(1)}, u32[]{:S(2)}, u32[]{:S(2)}) async-start(f32[32,8,128]{2,1,0:T(8,128)} %bitcast.9), calls=%async_computation.1 | async-start | bytes 262144 | tf_op jit(solution)/shard_map/all_to_all | solution.py:206
  36.5 0.0 copy-done.2
  36.5 0.1 add_bitcast_fusion
  36.6 0.6 %fusion.weight_ref = f32[4,8,8]{2,1,0:T(8,128)} fusion(f32[4,8]{1,0:T(4,128)S(1)} %fusion.2, s32[4,8]{1,0:T(4,128)S(1)} %add_bitcast_fusion), kind=kLoop, calls=%fused_computation.1 | loop fusion | flops 512 | bytes 1280 | tf_op jit(solution)/shard_map/jit(_where)/select_n | solution.py:211
  37.2 7.1 %all-to-all-done.1.got_ref = f32[32,8,128]{2,1,0:T(8,128)S(1)} async-done(((f32[32,8,128]{2,1,0:T(8,128)}), f32[32,8,128]{2,1,0:T(8,128)S(1)}, u32[]{:S(2)}, u32[]{:S(2)}) %all-to-all-start.1) | async-done | bytes 131104 | tf_op jit(solution)/shard_map/all_to_all | solution.py:206
  44.3 0.0 copy-start.1
  44.3 0.6 %copy-done.1 = f32[32,8,128]{2,1,0:T(8,128)} copy-done((f32[32,8,128]{2,1,0:T(8,128)}, f32[32,8,128]{2,1,0:T(8,128)S(1)}, u32[]{:S(2)}) %copy-start.1) | copy-done | bytes 131096
  45.0 1.6 %place.1 = f32[8,4,128]{2,1,0:T(4,128)} custom-call(f32[32,8,128]{2,1,0:T(8,128)} %copy-done.1, f32[4,8,8]{2,1,0:T(8,128)} %fusion.weight_ref), custom_call_target="tpu_custom_call" | custom-call | tf_op jit(solution)/shard_map/place/pallas_call | solution.py:151
Async XLA Ops:
  0.0 36.5 %copy-start.2 = (s32[6,4]{0,1:T(4,128)S(1)}, s32[6,4]{0,1:T(4,128)}, u32[]{:S(2)}) copy-start(s32[6,4]{0,1:T(4,128)} %param.10) | copy-start | bytes 292
  1.6 15.3 %all-to-all-start = ((s32[32,1,1280]{2,1,0:T(1,128)}), s32[32,1,1280]{2,1,0:T(1,128)S(1)}, u32[]{:S(2)}, u32[]{:S(2)}) async-start(s32[32,1,1280]{2,1,0:T(1,128)} %keys.1), calls=%async_computation | async-start | bytes 327680 | tf_op jit(solution)/shard_map/all_to_all | solution.py:203
  17.0 0.7 %copy-start = (s32[32,1,1280]{2,1,0:T(1,128)}, s32[32,1,1280]{2,1,0:T(1,128)S(1)}, u32[]{:S(2)}) copy-start(s32[32,1,1280]{2,1,0:T(1,128)S(1)} %all-to-all-done.ids_ref) | copy-start | bytes 491524
  33.7 10.7 %all-to-all-start.1 = ((f32[32,8,128]{2,1,0:T(8,128)}), f32[32,8,128]{2,1,0:T(8,128)S(1)}, u32[]{:S(2)}, u32[]{:S(2)}) async-start(f32[32,8,128]{2,1,0:T(8,128)} %bitcast.9), calls=%async_computation.1 | async-start | bytes 262144 | tf_op jit(solution)/shard_map/all_to_all | solution.py:206
  44.3 0.6 %copy-start.1 = (f32[32,8,128]{2,1,0:T(8,128)}, f32[32,8,128]{2,1,0:T(8,128)S(1)}, u32[]{:S(2)}) copy-start(f32[32,8,128]{2,1,0:T(8,128)S(1)} %all-to-all-done.1.got_ref) | copy-start | bytes 393220

commit v3 on v2

--- a/solution.py
+++ b/solution.py
@@ -131,7 +131,7 @@
         compiler_params=pltpu.CompilerParams(
             dimension_semantics=("arbitrary",), vmem_limit_bytes=56 * 2**20),
         name="pool",
-    )(row_base, ids, table)
+    )(row_base, pltpu.with_memory_space_constraint(ids, pltpu.VMEM), table)
 
 
 def place_kernel(got_ref, weight_ref, out_ref, *, tables, batch):
@@ -154,7 +154,7 @@
         in_specs=[pl.BlockSpec(memory_space=pltpu.VMEM), pl.BlockSpec(memory_space=pltpu.VMEM)],
         out_specs=pl.BlockSpec(memory_space=pltpu.VMEM),
         name="place",
-    )(got, weight)
+    )(pltpu.with_memory_space_constraint(got, pltpu.VMEM), weight)
 
 
 def key_kernel(short_len_ref, long_len_ref, short_ref, long_ref, out_ref, *, batch):

time: 47 us -> 44.6 us (0.949)
  local copies, waits for them, and re-layouts: 2.85 us -> 1.54 us
  Pallas kernels: 19.3 us -> 18.1 us
    unnamed x8 -> x4, local copies, waits for them, and re-layouts: 2.85 us -> 1.54 us
    pallas_call x1, Pallas kernels: 16 us -> 15.1 us  [pool(): pl.pallas_call(body, out_shape=jax.ShapeDtypeStruct((count * slots, dim),...]
  transfers between devices with their start and end apart: 2 -> 2, of which waited for: 2 -> 2; matrix products, arithmetic and copies ran while one was open for 6% -> 7% of each run, Pallas kernels for 0% -> 0%
where the time goes in v3:
time: 44.6 us; the launch traced here: 44.2 us
  Pallas kernels  18.1 us (41%)
  waiting for transfers between devices  12.8 us (29%)
  starting transfers between devices  10.2 us (23%)
  local copies, waits for them, and re-layouts  1.54 us (3%)
  other arithmetic  1.43 us (3%)
    pallas_call x1, Pallas kernels, pool(): pl.pallas_call(body, out_shape=jax.ShapeDtypeStruct((count * slots, dim),...  15.1 us
    all_to_all x1, starting transfers between devices, on_device(): ids = lax.all_to_all(sent, axes, split_axis=0, concat_axis=0, tiled=True)  7.33 us
    all_to_all x1, waiting for transfers between devices, on_device(): lax.all_to_all(part.reshape(devices, slots, part.shape[1]), axes, split_a...  7.12 us
    all_to_all x1, waiting for transfers between devices, on_device(): ids = lax.all_to_all(sent, axes, split_axis=0, concat_axis=0, tiled=True)  5.72 us
    all_to_all x1, starting transfers between devices, on_device(): lax.all_to_all(part.reshape(devices, slots, part.shape[1]), axes, split_a...  2.88 us
    pallas_call x1, Pallas kernels, make_keys(): pl.pallas_call(functools.partial(key_kernel, batch=batch), out_shape=jax....  1.61 us
    unnamed x4, local copies, waits for them, and re-layouts  1.54 us
    pallas_call x1, Pallas kernels, place(): pl.pallas_call(functools.partial(place_kernel, tables=tables, batch=batch...  1.45 us
  transfers between devices with their start and end apart: 2, of which 2 were waited for; matrix products, arithmetic and copies ran while one was open for 7% of the time, Pallas kernels for 0%

profile of v3, /device:TPU:0, one launch (start us, length us, event | category | flops | bytes accessed | tf_op | source)
XLA Modules:
  0.0 44.2 jit_solution(13588537329695787375)
XLA Ops:
  0.0 0.0 copy-start
  0.0 1.6 %keys.1 = s32[32,1,1280]{2,1,0:T(1,128)} custom-call(s32[4,6]{1,0:T(4,128)} %bitcast.10, s32[2,4]{1,0:T(2,128)} %long_len_ref.1, s32[6,4,32]{2,1,0:T(4,128)} %short_ref.1, s32[2,4,512]{2,1,0:T(4,128)} %long_ref.1), custom_call_target="tpu_custom_call" | custom-call | tf_op jit(solution)/shard_map/keys/pallas_call | solution.py:181
  1.6 7.3 %all-to-all-start = ((s32[32,1,1280]{2,1,0:T(1,128)}), s32[32,1,1280]{2,1,0:T(1,128)S(1)}, u32[]{:S(2)}, u32[]{:S(2)}) async-start(s32[32,1,1280]{2,1,0:T(1,128)} %keys.1), calls=%async_computation | async-start | bytes 327680 | tf_op jit(solution)/shard_map/all_to_all | solution.py:203
  9.0 0.8 %copy.9 = s32[2,4]{0,1:T(4,128)S(1)} copy(s32[2,4]{1,0:T(2,128)} %long_len_ref.1) | data formatting | bytes 64 | tf_op args[5]
  9.7 0.8 %copy.8 = s32[2,4]{0,1:T(4,128)S(1)} copy(s32[2,4]{1,0:T(2,128)} %param.13) | data formatting | bytes 64 | tf_op args[6]
  10.5 0.8 %fusion.2 = f32[4,8]{1,0:T(4,128)S(1)} fusion(s32[2,4]{0,1:T(4,128)S(1)} %copy.9, s32[6,4]{0,1:T(4,128)} %param.9), kind=kLoop, calls=%fused_computation.5 | loop fusion | flops 64 | bytes 256 | tf_op jit(solution)/shard_map/sqrt | solution.py:211
  11.2 5.7 %all-to-all-done.ids_ref = s32[32,1,1280]{2,1,0:T(1,128)S(1)} async-done(((s32[32,1,1280]{2,1,0:T(1,128)}), s32[32,1,1280]{2,1,0:T(1,128)S(1)}, u32[]{:S(2)}, u32[]{:S(2)}) %all-to-all-start) | async-done | bytes 163872 | tf_op jit(solution)/shard_map/all_to_all | solution.py:203
  17.0 15.1 %pool.1 = f32[256,128]{1,0:T(8,128)} custom-call(s32[1]{0:T(128)} %bitcast.base_ref, s32[32,1,1280]{2,1,0:T(1,128)S(1)} %all-to-all-done.ids_ref, bf16[32768,128]{1,0:T(8,128)(2,1)} %bitcast.8), custom_call_target="tpu_custom_call" | custom-call | tf_op jit(solution)/shard_map/pool/pallas_call | solution.py:116
  32.1 2.9 %all-to-all-start.1 = ((f32[32,8,128]{2,1,0:T(8,128)}), f32[32,8,128]{2,1,0:T(8,128)S(1)}, u32[]{:S(2)}, u32[]{:S(2)}) async-start(f32[32,8,128]{2,1,0:T(8,128)} %bitcast.9), calls=%async_computation.1 | async-start | bytes 262144 | tf_op jit(solution)/shard_map/all_to_all | solution.py:206
  34.9 0.0 copy-done
  34.9 0.1 add_bitcast_fusion
  35.0 0.6 %fusion.weight_ref = f32[4,8,8]{2,1,0:T(8,128)} fusion(f32[4,8]{1,0:T(4,128)S(1)} %fusion.2, s32[4,8]{1,0:T(4,128)S(1)} %add_bitcast_fusion), kind=kLoop, calls=%fused_computation.1 | loop fusion | flops 512 | bytes 1280 | tf_op jit(solution)/shard_map/jit(_where)/select_n | solution.py:211
  35.6 7.1 %all-to-all-done.1.got_ref = f32[32,8,128]{2,1,0:T(8,128)S(1)} async-done(((f32[32,8,128]{2,1,0:T(8,128)}), f32[32,8,128]{2,1,0:T(8,128)S(1)}, u32[]{:S(2)}, u32[]{:S(2)}) %all-to-all-start.1) | async-done | bytes 131104 | tf_op jit(solution)/shard_map/all_to_all | solution.py:206
  42.7 1.4 %place.1 = f32[8,4,128]{2,1,0:T(4,128)} custom-call(f32[32,8,128]{2,1,0:T(8,128)S(1)} %all-to-all-done.1.got_ref, f32[4,8,8]{2,1,0:T(8,128)} %fusion.weight_ref), custom_call_target="tpu_custom_call" | custom-call | tf_op jit(solution)/shard_map/place/pallas_call | solution.py:151
Async XLA Ops:
  0.0 34.9 %copy-start = (s32[6,4]{0,1:T(4,128)S(1)}, s32[6,4]{0,1:T(4,128)}, u32[]{:S(2)}) copy-start(s32[6,4]{0,1:T(4,128)} %param.10) | copy-start | bytes 292
  1.6 15.3 %all-to-all-start = ((s32[32,1,1280]{2,1,0:T(1,128)}), s32[32,1,1280]{2,1,0:T(1,128)S(1)}, u32[]{:S(2)}, u32[]{:S(2)}) async-start(s32[32,1,1280]{2,1,0:T(1,128)} %keys.1), calls=%async_computation | async-start | bytes 327680 | tf_op jit(solution)/shard_map/all_to_all | solution.py:203
  32.1 10.7 %all-to-all-start.1 = ((f32[32,8,128]{2,1,0:T(8,128)}), f32[32,8,128]{2,1,0:T(8,128)S(1)}, u32[]{:S(2)}, u32[]{:S(2)}) async-start(f32[32,8,128]{2,1,0:T(8,128)} %bitcast.9), calls=%async_computation.1 | async-start | bytes 262144 | tf_op jit(solution)/shard_map/all_to_all | solution.py:206
